TPU v7x, 32 devices: a whole 2x2x4 slice. The times are simulated.
32 devices in a mesh: replica: 4 (over y, core), shard: 8 (over z, x).
Axes of the slice: x: 2, y: 2, z: 4, core: 2. Of those that a mesh axis runs over, the one named last changes fastest.
Arguments:
- anchor: float32 [384, 8192], P('shard'), may hold values from -6 to 6
- replica_rows: bfloat16 [4, 384, 8192], P('replica', 'shard'), may hold values from -6 to 6
- outer_velocity: float32 [384, 8192], P('shard', 'replica'), may hold values from -6 to 6
- features: bfloat16 [4, 384, 256], P('replica', 'shard'), may hold values from -6 to 6
- cotangent: bfloat16 [4, 256, 1024], P('replica', 'shard'), may hold values from -0.375 to 0.375
- inner_weight: float32 [4, 384, 1024], P('replica', 'shard'), may hold values from -6 to 6
- first_moment: float32 [4, 384, 1024], P('replica', 'shard'), may hold values from -6 to 6
- second_moment: float32 [4, 384, 1024], P('replica', 'shard'), may hold values from 0.5 to 2
Outputs:
- new_anchor: float32 [384, 8192], P('shard')
- merged_rows: bfloat16 [4, 384, 8192], P('replica', 'shard')
- new_velocity: float32 [384, 8192], P('shard', 'replica')
- new_weight: float32 [4, 384, 1024], P('replica', 'shard')
- new_first: float32 [4, 384, 1024], P('replica', 'shard')
- new_second: float32 [4, 384, 1024], P('replica', 'shard')
All inputs are finite; a program needn't handle non-finite values.
Results may differ from a plain program's by a relative error of at most 0.0035.
Values may be sent and summed in bfloat16 or wider, within the bound.
A program may use at most 64 MiB of HBM per device.

v0:
```python
import jax
import jax.numpy as jnp
from jax import lax
from jax.sharding import PartitionSpec as P

momentum_keep = 0.9
outer_rate = 0.7
blend_keep = 0.5
inner_rate = 0.01
decay_first = 0.9
decay_second = 0.95
weight_decay = 0.1
epsilon = 1e-08
first_fix = 1.0 - 0.9**10
second_fix = 1.0 - 0.95**10


def outer_sync(anchor, replica_rows, outer_velocity):
    replicas = lax.axis_size("replica")
    own_rows = replica_rows[0].astype(jnp.float32)
    slice_width = outer_velocity.shape[1]
    offset = lax.axis_index("replica") * slice_width
    drift = anchor - own_rows
    summed = lax.psum(drift, "replica")
    velocity_all = lax.all_gather(
        outer_velocity.astype(jnp.bfloat16), "replica", axis=1, tiled=True
    ).astype(outer_velocity.dtype)
    outer_grad = summed / replicas
    velocity_next = momentum_keep * velocity_all + outer_grad
    new_anchor = anchor - outer_rate * (outer_grad + momentum_keep * velocity_next)
    new_velocity = lax.dynamic_slice_in_dim(velocity_next, offset, slice_width, 1)
    merged_rows = (blend_keep * own_rows + (1.0 - blend_keep) * new_anchor).astype(jnp.bfloat16)
    return (new_anchor, merged_rows[None], new_velocity)


def inner_update(features, cotangent, inner_weight, first_moment, second_moment):
    feature_rows = features[0]
    gradient = jnp.dot(
        feature_rows,
        lax.all_gather(cotangent, "shard", axis=1, tiled=True)[0],
        preferred_element_type=jnp.float32,
    )[None]
    new_first = decay_first * first_moment + (1.0 - decay_first) * gradient
    new_second = decay_second * second_moment + (1.0 - decay_second) * gradient * gradient
    stepped = new_first / first_fix / (jnp.sqrt(new_second / second_fix) + epsilon)
    new_weight = inner_weight - inner_rate * (stepped + weight_decay * inner_weight)
    return (new_weight, new_first, new_second)


def local(
    anchor,
    replica_rows,
    outer_velocity,
    features,
    cotangent,
    inner_weight,
    first_moment,
    second_moment,
):
    new_weight, new_first, new_second = inner_update(
        features, cotangent, inner_weight, first_moment, second_moment
    )
    new_anchor, merged_rows, new_velocity = outer_sync(anchor, replica_rows, outer_velocity)
    return (new_anchor, merged_rows, new_velocity, new_weight, new_first, new_second)


def solution(mesh):
    in_specs = (
        P("shard", None),
        P("replica", "shard", None),
        P("shard", "replica"),
        P("replica", "shard", None),
        P("replica", "shard", None),
        P("replica", "shard", None),
        P("replica", "shard", None),
        P("replica", "shard", None),
    )
    out_specs = (
        P("shard", None),
        P("replica", "shard", None),
        P("shard", "replica"),
        P("replica", "shard", None),
        P("replica", "shard", None),
        P("replica", "shard", None),
    )
    return jax.shard_map(local, mesh=mesh, in_specs=in_specs, out_specs=out_specs, check_vma=False)
```

profile of v0, /device:TPU:0, one launch (start us, length us, event | category | flops | bytes accessed | tf_op | source)
XLA Modules:
  0.0 71.8 jit_solution(1049866319276950009)
XLA Ops:
  7.2 0.0 copy-start
  7.2 0.0 all-reduce.2.cloned.1.call-start
  7.2 2.9 %convert_subtract_fusion = f32[48,8192]{1,0:T(8,128)} fusion(f32[48,8192]{1,0:T(8,128)} %param.8, bf16[1,48,8192]{2,1,0:T(8,128)(2,1)} %param.9), kind=kLoop, calls=%fused_computation.1 | loop fusion | flops 786432 | bytes 3932160 | tf_op jit(solution)/shard_map/sub | solution.py:23
  10.1 0.0 copy-start.3
  10.1 0.0 copy-start.7
  10.1 0.0 copy-start.4
  10.1 0.0 copy-start.5
  10.1 0.0 copy-start.6
  10.1 0.0 all-reduce.2.cloned.1.call-update
  10.2 0.9 %copy-done.3 = f32[48,2048]{1,0:T(8,128)S(1)} copy-done((f32[48,2048]{1,0:T(8,128)S(1)}, f32[48,2048]{1,0:T(8,128)}, u32[]{:S(2)}) %copy-start.3) | copy-done | bytes 393240
  11.1 0.0 copy-done.7
  11.1 0.0 copy-start.1
  11.2 0.0 copy-start.2
  11.2 33.3 %all_gather.7 = bf16[1,256,1024]{2,1,0:T(8,128)(2,1)S(1)} all-gather(bf16[1,32,1024]{2,1,0:T(8,128)(2,1)S(1)} %copy-done.7), channel_id=1, replica_groups=mesh['replica'=4,'shard'=8] {'shard'}, dimensions={1}, use_global_device_ids=true | all-gather | bytes 589824 | tf_op jit(solution)/shard_map/all_gather | solution.py:40
  44.4 0.0 copy-done
  44.4 0.0 copy-done.4
  44.4 0.0 copy-done.5
  44.5 0.0 copy-done.6
  44.5 1.1 %multiply_subtract_fusion.1 = (f32[1,48,1024]{2,1,0:T(8,128)}, f32[1,48,1024]{2,1,0:T(8,128)}, f32[1,48,1024]{2,1,0:T(8,128)}) fusion(f32[1,48,1024]{2,1,0:T(8,128)S(1)} %copy-done.4, f32[1,48,1024]{2,1,0:T(8,128)S(1)} %copy-done.5, f32[1,48,1024]{2,1,0:T(8,128)S(1)} %copy-done.6, bf16[1,256,1024]{2,1,0:T(8,128)(2,1)S(1)} %all_gather.7, ...), kind=kOutput, calls=%fused_computation.13 | convolution fusion | flops 25903104 | bytes 1728512 | tf_op jit(solution)/shard_map/dot_general | solution.py:38
  45.6 13.3 %all_gather.6 = bf16[48,8192]{1,0:T(8,128)(2,1)S(1)} all-gather(bf16[48,2048]{1,0:T(8,128)(2,1)S(1)} %convert_element_type.17), channel_id=1, replica_groups=mesh['replica'=4,'shard'=8] {'replica'}, dimensions={1}, use_global_device_ids=true | all-gather | bytes 983040 | tf_op jit(solution)/shard_map/all_gather | solution.py:25
  58.9 1.9 %all-reduce.2.cloned.1.call-done = f32[48,8192]{1,0:T(8,128)} async-done(((f32[48,8192]{1,0:T(8,128)}), f32[48,8192]{1,0:T(8,128)}) %all-reduce.2.cloned.1.call-update) | async-done | bytes 1572880 | tf_op jit(solution)/shard_map/psum | solution.py:24
  60.8 0.0 copy-done.1
  60.8 0.0 copy-done.2
  60.8 3.4 %fusion.2 = (bf16[1,48,8192]{2,1,0:T(8,128)(2,1)}, f32[48,8192]{1,0:T(8,128)}, f32[48,8192]{1,0:T(8,128)S(1)}) fusion(bf16[1,48,8192]{2,1,0:T(8,128)(2,1)S(1)} %copy-done.2, f32[48,8192]{1,0:T(8,128)S(1)} %copy-done.1, bf16[48,8192]{1,0:T(8,128)(2,1)S(1)} %all_gather.6, f32[48,8192]{1,0:T(8,128)} %all-reduce.2.cloned.1.call-done), kind=kLoop, calls=%fused_computation.6 | loop fusion | flops 4718592 | bytes 8650752 | tf_op jit(solution)/shard_map/broadcast_in_dim | solution.py:33
  64.2 0.8 %constant_dynamic-slice_fusion = f32[48,2048]{1,0:T(8,128)} fusion(f32[48,8192]{1,0:T(8,128)S(1)} %get-tuple-element.11, s32[]{:T(128)S(6)} %select_n.3), kind=kLoop, calls=%fused_computation.15 | loop fusion | bytes 786436 | tf_op jit(solution)/shard_map/dynamic_slice | solution.py:31
  (1 shorter events, 0.0 us)
Async XLA Ops:
  7.2 37.3 %copy-start = (bf16[1,48,256]{2,1,0:T(8,128)(2,1)S(1)}, bf16[1,48,256]{2,1,0:T(8,128)(2,1)}, u32[]{:S(2)}) copy-start(bf16[1,48,256]{2,1,0:T(8,128)(2,1)} %param.11) | copy-start | bytes 73732
  7.2 53.6 %all-reduce.2.cloned.1.call-start = ((), (), s32[]{:S(2)}) async-start(), calls=%async_computation | async-start | bytes 3145728 | tf_op jit(solution)/shard_map/psum | solution.py:24
  10.1 1.0 %copy-start.3 = (f32[48,2048]{1,0:T(8,128)S(1)}, f32[48,2048]{1,0:T(8,128)}, u32[]{:S(2)}) copy-start(f32[48,2048]{1,0:T(8,128)} %param.10) | copy-start | bytes 1179652
  10.1 1.0 %copy-start.7 = (bf16[1,32,1024]{2,1,0:T(8,128)(2,1)S(1)}, bf16[1,32,1024]{2,1,0:T(8,128)(2,1)}, u32[]{:S(2)}) copy-start(bf16[1,32,1024]{2,1,0:T(8,128)(2,1)} %param.12) | copy-start | bytes 196612
  10.1 34.3 %copy-start.4 = (f32[1,48,1024]{2,1,0:T(8,128)S(1)}, f32[1,48,1024]{2,1,0:T(8,128)}, u32[]{:S(2)}) copy-start(f32[1,48,1024]{2,1,0:T(8,128)} %param.13) | copy-start | bytes 589828
  10.1 34.3 %copy-start.5 = (f32[1,48,1024]{2,1,0:T(8,128)S(1)}, f32[1,48,1024]{2,1,0:T(8,128)}, u32[]{:S(2)}) copy-start(f32[1,48,1024]{2,1,0:T(8,128)} %param.14) | copy-start | bytes 589828
  10.1 34.3 %copy-start.6 = (f32[1,48,1024]{2,1,0:T(8,128)S(1)}, f32[1,48,1024]{2,1,0:T(8,128)}, u32[]{:S(2)}) copy-start(f32[1,48,1024]{2,1,0:T(8,128)} %param.15) | copy-start | bytes 589828
  11.1 49.6 %copy-start.1 = (f32[48,8192]{1,0:T(8,128)S(1)}, f32[48,8192]{1,0:T(8,128)}, u32[]{:S(2)}) copy-start(f32[48,8192]{1,0:T(8,128)} %param.8) | copy-start | bytes 4718596
  11.2 49.6 %copy-start.2 = (bf16[1,48,8192]{2,1,0:T(8,128)(2,1)S(1)}, bf16[1,48,8192]{2,1,0:T(8,128)(2,1)}, u32[]{:S(2)}) copy-start(bf16[1,48,8192]{2,1,0:T(8,128)(2,1)} %param.9) | copy-start | bytes 2359300
Sparse Core Ops, SparseCore 0:
  10.9 49.7 all-reduce.1
where the time goes:
time: 72 us; the launch traced here: 71.8 us
  blocking collectives  46.6 us (65%)
  between operations  14.1 us (20%)
  other arithmetic  6.34 us (9%)
  waiting for transfers between devices  1.87 us (3%)
  local copies, waits for them, and re-layouts  1.75 us (2%)
  matrix products  1.11 us (2%)
    all_gather x1, blocking collectives, inner_update(): lax.all_gather(cotangent, 'shard', axis=1, tiled=True)[0]  33.3 us
    all_gather x1, blocking collectives, outer_sync(): lax.all_gather(outer_velocity.astype(jnp.bfloat16), 'replica', axis=1, ti...  13.3 us
    broadcast_in_dim x1, other arithmetic, outer_sync(): return (new_anchor, merged_rows[None], new_velocity)  3.43 us
    sub x1, other arithmetic, outer_sync(): drift = anchor - own_rows  2.88 us
    psum x1, waiting for transfers between devices, outer_sync(): summed = lax.psum(drift, 'replica')  1.86 us
  transfers between devices with their start and end apart: 1, of which 1 were waited for; matrix products, arithmetic and copies ran while one was open for 2% of the time, Pallas kernels for 0%

commit v1 on v0

--- a/solution.py
+++ b/solution.py
@@ -22,8 +22,8 @@
     offset = lax.axis_index("replica") * slice_width
     drift = anchor - own_rows
     summed = lax.psum(drift, "replica")
-    velocity_all = lax.all_gather(
-        outer_velocity.astype(jnp.bfloat16), "replica", axis=1, tiled=True
+    velocity_all = jnp.concatenate(
+        lax.all_gather(outer_velocity.astype(jnp.bfloat16), "replica"), axis=1
     ).astype(outer_velocity.dtype)
     outer_grad = summed / replicas
     velocity_next = momentum_keep * velocity_all + outer_grad

time: 72 us -> 69.1 us (0.960)
  blocking collectives: 46.6 us -> 42.1 us
  local copies, waits for them, and re-layouts: 1.75 us -> 3.68 us
  waiting for transfers between devices: 1.87 us -> 0.02 us
  matrix products: 1.11 us -> 2.13 us
    all_gather x1, blocking collectives: 13.3 us -> 10.1 us  [outer_sync(): lax.all_gather(outer_velocity.astype(jnp.bfloat16), 'replica')]
    psum x1, waiting for transfers between devices: 1.86 us -> 0.01 us  [outer_sync(): summed = lax.psum(drift, 'replica')]
    all_gather x1, blocking collectives: 33.3 us -> 32 us  [inner_update(): lax.all_gather(cotangent, 'shard', axis=1, tiled=True)[0]]
    dot_general x1, matrix products: 1.11 us -> 2.13 us  [inner_update(): jnp.dot(feature_rows, lax.all_gather(cotangent, 'shard', axis=1, tiled=Tr...]
    mul x0 -> x1, local copies, waits for them, and re-layouts: none -> 1.01 us  [outer_sync(): velocity_next = momentum_keep * velocity_all + outer_grad]
    unnamed x16 -> x11, local copies, waits for them, and re-layouts: 0.98 us -> 1.9 us
  transfers between devices with their start and end apart: 1 -> 1, of which waited for: 1 -> 0; matrix products, arithmetic and copies ran while one was open for 2% -> 6% of each run, Pallas kernels for 0% -> 0%
where the time goes in v1:
time: 69.1 us; the launch traced here: 68.8 us
  blocking collectives  42.1 us (61%)
  between operations  14.1 us (20%)
  other arithmetic  6.73 us (10%)
  local copies, waits for them, and re-layouts  3.68 us (5%)
  matrix products  2.13 us (3%)
    all_gather x1, blocking collectives, inner_update(): lax.all_gather(cotangent, 'shard', axis=1, tiled=True)[0]  32 us
    all_gather x1, blocking collectives, outer_sync(): lax.all_gather(outer_velocity.astype(jnp.bfloat16), 'replica')  10.1 us
    broadcast_in_dim x1, other arithmetic, outer_sync(): return (new_anchor, merged_rows[None], new_velocity)  3.65 us
    sub x1, other arithmetic, outer_sync(): drift = anchor - own_rows  2.88 us
    dot_general x1, matrix products, inner_update(): jnp.dot(feature_rows, lax.all_gather(cotangent, 'shard', axis=1, tiled=Tr...  2.13 us
    unnamed x11, local copies, waits for them, and re-layouts  1.9 us
  transfers between devices with their start and end apart: 1, of which 0 were waited for; matrix products, arithmetic and copies ran while one was open for 6% of the time, Pallas kernels for 0%

profile of v1, /device:TPU:0, one launch (start us, length us, event | category | flops | bytes accessed | tf_op | source)
XLA Modules:
  0.0 68.8 jit_solution(16332375424898994133)
XLA Ops:
  7.2 0.0 copy-start
  7.2 0.0 all-reduce.2.cloned.1.call-start
  7.2 2.9 %convert_subtract_fusion = f32[48,8192]{1,0:T(8,128)} fusion(f32[48,8192]{1,0:T(8,128)} %param.8, bf16[1,48,8192]{2,1,0:T(8,128)(2,1)} %param.9), kind=kLoop, calls=%fused_computation.1 | loop fusion | flops 786432 | bytes 3932160 | tf_op jit(solution)/shard_map/sub | solution.py:23
  10.1 0.0 copy-start.2
  10.1 0.0 all-reduce.2.cloned.1.call-update
  10.1 1.0 %copy-done.2 = f32[48,2048]{1,0:T(8,128)S(1)} copy-done((f32[48,2048]{1,0:T(8,128)S(1)}, f32[48,2048]{1,0:T(8,128)}, u32[]{:S(2)}) %copy-start.2) | copy-done | bytes 393240
  11.1 10.1 %all-gather = bf16[192,2048]{1,0:T(8,128)(2,1)S(1)} all-gather(bf16[48,2048]{1,0:T(8,128)(2,1)S(1)} %convert_element_type.19), channel_id=2, replica_groups=mesh['replica'=4,'shard'=8] {'replica'}, dimensions={0}, use_global_device_ids=true | all-gather | bytes 983040 | tf_op jit(solution)/shard_map/all_gather | solution.py:26
  21.2 0.2 convert_multiply_fusion
  21.4 1.0 %copy.14 = f32[4,48,2048]{2,0,1:T(4,128)S(1)} copy(f32[4,48,2048]{2,1,0:T(8,128)S(1)} %bitcast.29) | data formatting | bytes 3145728 | tf_op jit(solution)/shard_map/mul | solution.py:29
  22.4 0.0 copy-start.4
  22.5 0.0 copy-start.3
  22.5 0.9 %copy.15 = f32[6,8,4,2048]{3,1,2,0:T(8,128)S(1)} copy(f32[6,8,4,2048]{3,2,1,0:T(4,128)S(1)} %bitcast.30) | data formatting | bytes 3145728
  23.4 0.0 copy-start.1
  23.4 0.0 copy-done.4
  23.4 32.0 %all_gather.11 = bf16[1,256,1024]{2,1,0:T(8,128)(2,1)S(1)} all-gather(bf16[1,32,1024]{2,1,0:T(8,128)(2,1)S(1)} %copy-done.4), channel_id=1, replica_groups=mesh['replica'=4,'shard'=8] {'shard'}, dimensions={1}, use_global_device_ids=true | all-gather | bytes 589824 | tf_op jit(solution)/shard_map/all_gather | solution.py:40
  55.4 0.0 copy-done
  55.4 0.0 copy-done.3
  55.4 2.1 %multiply_subtract_fusion.1 = (f32[1,48,1024]{2,1,0:T(8,128)}, f32[1,48,1024]{2,1,0:T(8,128)}, f32[1,48,1024]{2,1,0:T(8,128)}) fusion(f32[1,48,1024]{2,1,0:T(8,128)S(1)} %copy-done.3, f32[1,48,1024]{2,1,0:T(8,128)} %param.14, f32[1,48,1024]{2,1,0:T(8,128)} %param.15, bf16[1,256,1024]{2,1,0:T(8,128)(2,1)S(1)} %all_gather.11, bf16[1,48,256]{2,1,0:T(8,128)(2,1)S(1)} %copy-done), kind=kOutput, calls=%fused_computation.14 | convolution fusion | flops 25903104 | bytes 1728512 | tf_op jit(solution)/shard_map/dot_general | solution.py:38
  57.5 0.0 all-reduce.2.cloned.1.call-done
  57.5 0.0 copy-done.1
  57.5 3.6 %fusion.2 = (bf16[1,48,8192]{2,1,0:T(8,128)(2,1)}, f32[48,8192]{1,0:T(8,128)}, f32[48,8192]{1,0:T(8,128)S(1)}) fusion(bf16[1,48,8192]{2,1,0:T(8,128)(2,1)} %param.9, f32[48,8192]{1,0:T(8,128)S(1)} %copy-done.1, f32[48,8192]{1,0:T(8,128)S(1)} %bitcast.28, f32[48,8192]{1,0:T(8,128)} %all-reduce.2.cloned.1.call-done), kind=kLoop, calls=%fused_computation.7 | loop fusion | flops 3932160 | bytes 9437184 | tf_op jit(solution)/shard_map/broadcast_in_dim | solution.py:33
  61.2 0.8 %constant_dynamic-slice_fusion = f32[48,2048]{1,0:T(8,128)} fusion(f32[48,8192]{1,0:T(8,128)S(1)} %get-tuple-element.11, s32[]{:T(128)S(6)} %select_n.3), kind=kLoop, calls=%fused_computation.16 | loop fusion | bytes 786436 | tf_op jit(solution)/shard_map/dynamic_slice | solution.py:31
  (1 shorter events, 0.0 us)
Async XLA Ops:
  7.2 48.2 %copy-start = (bf16[1,48,256]{2,1,0:T(8,128)(2,1)S(1)}, bf16[1,48,256]{2,1,0:T(8,128)(2,1)}, u32[]{:S(2)}) copy-start(bf16[1,48,256]{2,1,0:T(8,128)(2,1)} %param.11) | copy-start | bytes 73732
  7.2 50.4 %all-reduce.2.cloned.1.call-start = ((), (), s32[]{:S(2)}) async-start(), calls=%async_computation | async-start | bytes 3145728 | tf_op jit(solution)/shard_map/psum | solution.py:24
  10.1 1.0 %copy-start.2 = (f32[48,2048]{1,0:T(8,128)S(1)}, f32[48,2048]{1,0:T(8,128)}, u32[]{:S(2)}) copy-start(f32[48,2048]{1,0:T(8,128)} %param.10) | copy-start | bytes 1179652
  22.4 1.0 %copy-start.4 = (bf16[1,32,1024]{2,1,0:T(8,128)(2,1)S(1)}, bf16[1,32,1024]{2,1,0:T(8,128)(2,1)}, u32[]{:S(2)}) copy-start(bf16[1,32,1024]{2,1,0:T(8,128)(2,1)} %param.12) | copy-start | bytes 196612
  22.5 33.0 %copy-start.3 = (f32[1,48,1024]{2,1,0:T(8,128)S(1)}, f32[1,48,1024]{2,1,0:T(8,128)}, u32[]{:S(2)}) copy-start(f32[1,48,1024]{2,1,0:T(8,128)} %param.13) | copy-start | bytes 589828
  23.4 34.2 %copy-start.1 = (f32[48,8192]{1,0:T(8,128)S(1)}, f32[48,8192]{1,0:T(8,128)}, u32[]{:S(2)}) copy-start(f32[48,8192]{1,0:T(8,128)} %param.8) | copy-start | bytes 4718596
Sparse Core Ops, SparseCore 0:
  10.9 45.6 all-reduce.1
